TPU v7x, 32 devices: a whole 2x2x4 slice. The times are simulated.
32 devices in a mesh: ctx: 2 (over x), tp: 4 (over y, core), dp: 4 (over z).
Axes of the slice: x: 2, y: 2, z: 4, core: 2. Of those that a mesh axis runs over, the one named last changes fastest.
Arguments:
- hidden: bfloat16 [4, 1024, 4096], P('dp', 'ctx', 'tp'), may hold values from -6 to 6
- target: bfloat16 [4, 1024, 4096], P('dp', 'ctx', 'tp'), may hold values from -24 to 24
- gain: float32 [4096], replicated, may hold values from 0.5 to 1.5
- w_query: bfloat16 [4096, 2048], P(('ctx', 'dp'), 'tp'), may hold values from -2.15625 to 2.15625
- w_key: bfloat16 [4096, 512], P(('ctx', 'dp'), 'tp'), may hold values from -0.09375 to 0.09375
- value_matrix: bfloat16 [4096, 512], P(('ctx', 'dp'), 'tp'), may hold values from -0.09375 to 0.09375
- w_out: bfloat16 [2048, 4096], P('tp', ('ctx', 'dp')), may hold values from -0.125 to 0.125
- block_order: int32 [4], replicated, may hold values from 0 to 3, each once
Outputs:
- branch: bfloat16 [4, 1024, 4096], P('dp', 'ctx', 'tp')
- loss: float32 [], replicated
Inputs may be any that keep to these rules, and one draw needn't show every extreme that they name: block_order is a permutation of 0 to 3.
All inputs are finite; a program needn't handle non-finite values.
Results may differ from a plain program's by a relative error of at most 0.013.
The roundings to bfloat16 on the way count: a program that leaves them out, or rounds other values in their place, can miss the bound.
Values may be sent and summed in bfloat16 or wider, within the bound.
A program may use at most 128 MiB of HBM per device.

v0:
```python
import jax
import jax.numpy as jnp
from jax import lax
from jax.sharding import PartitionSpec as P

MODEL_WIDTH = 4096
QUERY_HEADS = 16
KEY_VALUE_HEADS = 4
HEAD_SIZE = 128
rope_base = 500000.0


def shifted(value, axis, by):
    peers = lax.axis_size(axis)
    return lax.ppermute(value, axis, [(i, (i + by) % peers) for i in range(peers)])


def positions(order, start, rows, half):
    index = start + lax.iota(jnp.int32, rows)
    block = index // half
    slots = lax.iota(jnp.int32, order.shape[0])
    chosen = jnp.sum(jnp.where(block[:, None] == slots[None, :], order[None, :], 0), axis=1)
    return chosen * half + index % half


def apply_rotary(values, token_places):
    half = values.shape[-1] // 2
    freqs = rope_base ** (-(jnp.arange(half, dtype=jnp.float32) * 2.0) / values.shape[-1])
    angles = token_places.astype(jnp.float32)[:, None] * freqs[None, :]
    cosine = jnp.cos(angles)[:, None, :]
    sine = jnp.sin(angles)[:, None, :]
    first = values[..., :half]
    second = values[..., half:]
    return jnp.concatenate(
        [first * cosine - second * sine, second * cosine + first * sine], axis=-1
    )


def attend(state, query_rows, qpos, piece, kpos):
    peak, total, accum = state
    rows = piece.shape[1]
    local_heads = query_rows.shape[1]
    pair = piece.reshape(2, rows, local_heads, HEAD_SIZE)
    scores = jnp.einsum(
        "qcgd,kcd->cgqk", query_rows, pair[0], preferred_element_type=jnp.float32
    ) * (1.0 / HEAD_SIZE**0.5)
    allowed = (qpos[:, None] >= kpos[None, :])[None, None]
    scores = jnp.where(allowed, scores, -1e30)
    new_peak = jnp.maximum(peak, jnp.max(scores, axis=-1))
    weights = jnp.where(allowed, jnp.exp(scores - new_peak[..., None]), 0.0)
    factor = jnp.exp(peak - new_peak)
    total = total * factor + jnp.sum(weights, axis=-1)
    update = jnp.einsum(
        "cgqk,kcd->qcgd", weights.astype(jnp.bfloat16), pair[1], preferred_element_type=jnp.float32
    )
    accum = accum * jnp.transpose(factor, (2, 0, 1))[..., None] + update
    return (new_peak, total, accum)


def on_device(hidden, target, gain, w_query, w_key, value_matrix, w_out, block_order):
    rows = hidden.shape[1]
    half = rows // 2
    local = hidden[0]
    whole = lax.all_gather(local, "tp", axis=1, tiled=True)
    wide = whole.astype(jnp.float32)
    normed = (
        wide * lax.rsqrt(jnp.mean(wide * wide, axis=1, keepdims=True) + 1e-05) * gain[None, :]
    ).astype(jnp.bfloat16)
    pieces = (
        lax.all_gather(w_query, ("ctx", "dp"), axis=0, tiled=True),
        lax.all_gather(w_key, ("ctx", "dp"), axis=0, tiled=True),
        lax.all_gather(value_matrix, ("ctx", "dp"), axis=0, tiled=True),
    )
    query_rows, key, value_rows = tuple(
        (jnp.dot(normed, piece, preferred_element_type=jnp.float32) for piece in pieces)
    )
    shard = lax.axis_index("ctx")
    qpos = positions(block_order, shard * rows, rows, half)
    local_heads = w_key.shape[1] // HEAD_SIZE
    query_group = QUERY_HEADS // KEY_VALUE_HEADS
    query_rows = (
        apply_rotary(query_rows.reshape(rows, local_heads * query_group, HEAD_SIZE), qpos)
        .astype(jnp.bfloat16)
        .reshape(rows, local_heads, query_group, HEAD_SIZE)
    )
    key = (
        apply_rotary(key.reshape(rows, local_heads, HEAD_SIZE), qpos)
        .astype(jnp.bfloat16)
        .reshape(rows, local_heads * HEAD_SIZE)
    )
    pair = jnp.stack([key, value_rows.astype(jnp.bfloat16)])
    state = (
        jnp.full((local_heads, query_group, rows), -1e30, jnp.float32),
        jnp.zeros((local_heads, query_group, rows), jnp.float32),
        jnp.zeros((rows, local_heads, query_group, HEAD_SIZE), jnp.float32),
    )
    count = lax.axis_size("ctx")
    state = attend(state, query_rows, qpos, pair, qpos)

    def turn(step, carry):
        moved, inner = carry
        moved = shifted(moved, "ctx", 1)
        source = (shard - step) % count
        return (
            moved,
            attend(
                inner, query_rows, qpos, moved, positions(block_order, source * rows, rows, half)
            ),
        )

    moved_end, state = lax.fori_loop(1, count, turn, (pair, state))
    peak, total, accum = state
    attn = (
        (accum / jnp.transpose(total, (2, 0, 1))[..., None])
        .astype(jnp.bfloat16)
        .reshape(rows, local_heads * query_group * HEAD_SIZE)
    )
    terms = jnp.dot(
        attn,
        lax.all_gather(w_out, ("ctx", "dp"), axis=1, tiled=True),
        preferred_element_type=jnp.float32,
    )
    summed = lax.psum_scatter(terms.astype(jnp.bfloat16), "tp", scatter_dimension=1, tiled=True)
    resid = local.astype(jnp.float32) + summed.astype(jnp.float32) - target[0].astype(jnp.float32)
    squares = lax.psum(jnp.sum(resid * resid), ("ctx", "tp", "dp"))
    loss = squares / (lax.axis_size("dp") * lax.axis_size("ctx") * rows * MODEL_WIDTH)
    return (summed[None], loss)


def solution(mesh):
    in_specs = (
        P("dp", "ctx", "tp"),
        P("dp", "ctx", "tp"),
        P(),
        P(("ctx", "dp"), "tp"),
        P(("ctx", "dp"), "tp"),
        P(("ctx", "dp"), "tp"),
        P("tp", ("ctx", "dp")),
        P(),
    )
    out_specs = (P("dp", "ctx", "tp"), P())
    return jax.shard_map(
        on_device, mesh=mesh, in_specs=in_specs, out_specs=out_specs, check_vma=False
    )
```

profile of v0, /device:TPU:0, one launch (start us, length us, event | category | flops | bytes accessed | tf_op | source)
XLA Modules:
  0.0 378.8 jit_solution(6131819200116777629)
XLA Ops:
  7.2 0.7 all-gather.15.cloned.1.call-update
  8.0 0.7 all-gather.7.cloned.1.call-update
  8.7 0.7 all-gather.11.cloned.1.call-update
  9.4 0.5 all-gather.9.cloned.1.call-update
  10.0 0.5 all-gather.13.cloned.1.call-update
  10.7 0.7 select_reduce_fusion
  11.4 1.8 multiply_cosine_fusion
  13.2 0.4 broadcast_compare_fusion
  13.6 33.2 %all-gather.15.cloned.1.call-done = bf16[1,512,4096]{2,1,0:T(8,128)(2,1)} async-done(((bf16[1,512,1024]{2,1,0:T(8,128)(2,1)}), bf16[1,512,4096]{2,1,0:T(8,128)(2,1)}) %all-gather.15.cloned.1.call-update) | async-done | bytes 4194320 | tf_op jit(solution)/shard_map/all_gather | solution.py:64
  46.8 3.1 fusion
  49.9 39.3 %all-gather.7.cloned.1.call-done = bf16[4096,128]{1,0:T(8,128)(2,1)} async-done(((bf16[512,128]{1,0:T(8,128)(2,1)}), bf16[4096,128]{1,0:T(8,128)(2,1)}) %all-gather.7.cloned.1.call-update) | async-done | bytes 1048592 | tf_op jit(solution)/shard_map/all_gather | solution.py:71
  89.2 4.1 %convolution_bitcast_fusion = f32[512,1,128]{0,2,1:T(8,128)S(1)} fusion(bf16[4096,128]{1,0:T(8,128)(2,1)} %all-gather.7.cloned.1.call-done, bf16[1,512,4096]{2,1,0:T(8,128)(2,1)} %all-gather.15.cloned.1.call-done, f32[4096]{0:T(1024)S(1)} %copy-done.4, f32[512]{0:T(512)S(1)} %add_rsqrt_fusion), kind=kOutput, calls=%fused_computation.31 | convolution fusion | flops 545259520 | bytes 5523456 | tf_op jit(solution)/shard_map/dot_general | solution.py:75
  93.3 0.6 fusion.41
  93.9 36.5 %all-gather.11.cloned.1.call-done = bf16[4096,128]{1,0:T(8,128)(2,1)} async-done(((bf16[512,128]{1,0:T(8,128)(2,1)}), bf16[4096,128]{1,0:T(8,128)(2,1)}) %all-gather.11.cloned.1.call-update) | async-done | bytes 1048592 | tf_op jit(solution)/shard_map/all_gather | solution.py:72
  130.4 4.1 %convolution_convert_fusion.1 = bf16[512,128]{0,1:T(8,128)(2,1)S(1)} fusion(bf16[4096,128]{1,0:T(8,128)(2,1)} %all-gather.11.cloned.1.call-done, bf16[1,512,4096]{2,1,0:T(8,128)(2,1)} %all-gather.15.cloned.1.call-done, f32[4096]{0:T(1024)S(1)} %copy-done.4, f32[512]{0:T(512)S(1)} %add_rsqrt_fusion), kind=kOutput, calls=%fused_computation.32 | convolution fusion | flops 545325056 | bytes 5392384 | tf_op jit(solution)/shard_map/dot_general | solution.py:75
  134.5 0.8 pad_maximum_fusion.1
  135.3 0.6 collective-permute-start
  135.9 68.1 %all-gather.9.cloned.1.call-done = bf16[4096,512]{1,0:T(8,128)(2,1)} async-done(((bf16[512,512]{1,0:T(8,128)(2,1)}), bf16[4096,512]{1,0:T(8,128)(2,1)}) %all-gather.9.cloned.1.call-update) | async-done | bytes 4194320 | tf_op jit(solution)/shard_map/all_gather | solution.py:70
  203.9 5.9 %fusion.74 = f32[512,512]{0,1:T(8,128)S(1)} fusion(bf16[4096,512]{1,0:T(8,128)(2,1)} %all-gather.9.cloned.1.call-done, bf16[1,512,4096]{2,1,0:T(8,128)(2,1)} %all-gather.15.cloned.1.call-done, f32[4096]{0:T(1024)S(1)} %copy-done.4, f32[512]{0:T(512)S(1)} %add_rsqrt_fusion), kind=kOutput, calls=%fused_computation.109 | convolution fusion | flops 2155872256 | bytes 9455616 | tf_op jit(solution)/shard_map/dot_general | solution.py:75
  210.3 0.3 copy.32
  210.6 1.2 subtract_convert_fusion
  211.9 1.2 fusion.3
  213.1 2.1 fusion.4
  215.3 1.0 fusion.5
  216.3 1.2 fusion.7
  217.6 1.3 fusion.28
  218.9 2.2 divide_convert_fusion
  221.1 57.8 %all-gather.13.cloned.1.call-done = bf16[512,4096]{1,0:T(8,128)(2,1)} async-done(((bf16[512,512]{1,0:T(8,128)(2,1)}), bf16[512,4096]{1,0:T(8,128)(2,1)}) %all-gather.13.cloned.1.call-update) | async-done | bytes 4194320 | tf_op jit(solution)/shard_map/all_gather | solution.py:120
  279.0 6.5 %convolution_convert_fusion = bf16[512,4096]{1,0:T(8,128)(2,1)} fusion(bf16[512,512]{0,1:T(8,128)(2,1)S(1)} %bitcast.172, bf16[512,4096]{1,0:T(8,128)(2,1)} %all-gather.13.cloned.1.call-done), kind=kOutput, calls=%fused_computation.5 | convolution fusion | flops 2149580800 | bytes 8912896 | tf_op jit(solution)/shard_map/dot_general | solution.py:118
  285.6 42.7 %reduce-scatter.2.cloned.1.call-done = bf16[512,1024]{1,0:T(8,128)(2,1)} async-done(((bf16[512,4096]{1,0:T(8,128)(2,1)}), bf16[512,1024]{1,0:T(8,128)(2,1)}) %reduce-scatter.2.cloned.1.call-update) | async-done | bytes 1048592 | tf_op jit(solution)/shard_map/reduce_scatter | solution.py:123
  328.3 2.4 fusion.12
  330.7 39.5 %psum.7 = f32[]{:T(128)} all-reduce(f32[]{:T(128)} %fusion.12), channel_id=1, replica_groups=mesh['ctx'=2,'tp'=4,'dp'=4] {'ctx','tp','dp'}, use_global_device_ids=true, to_apply=%region_9.10 | all-reduce | flops 1 | bytes 8 | tf_op jit(solution)/shard_map/psum | solution.py:125
  (27 shorter events, 0.8 us)
Async XLA Ops:
  7.2 82.0 %copy-start.4 = (f32[4096]{0:T(1024)S(1)}, f32[4096]{0:T(1024)}, u32[]{:S(2)}) copy-start(f32[4096]{0:T(1024)} %param.10) | copy-start | bytes 49156
  7.2 39.6 %all-gather.15.cloned.1.call-start = ((), (), s32[]{:S(2)}) async-start(), calls=%async_computation.6 | async-start | bytes 5242880 | tf_op jit(solution)/shard_map/all_gather | solution.py:64
  7.9 81.3 %all-gather.7.cloned.1.call-start = ((), (), s32[]{:S(2)}) async-start(), calls=%async_computation.1 | async-start | bytes 1179648 | tf_op jit(solution)/shard_map/all_gather | solution.py:71
  8.7 121.8 %all-gather.11.cloned.1.call-start = ((), (), s32[]{:S(2)}) async-start(), calls=%async_computation.3 | async-start | bytes 1179648 | tf_op jit(solution)/shard_map/all_gather | solution.py:72
  9.4 194.5 %all-gather.9.cloned.1.call-start = ((), (), s32[]{:S(2)}) async-start(), calls=%async_computation.2 | async-start | bytes 4718592 | tf_op jit(solution)/shard_map/all_gather | solution.py:70
  10.0 269.0 %all-gather.13.cloned.1.call-start = ((), (), s32[]{:S(2)}) async-start(), calls=%async_computation.4 | async-start | bytes 4718592 | tf_op jit(solution)/shard_map/all_gather | solution.py:120
  10.6 317.7 %reduce-scatter.2.cloned.1.call-start = ((), (), s32[]{:S(2)}) async-start(), calls=%async_computation.5 | async-start | bytes 5242880 | tf_op jit(solution)/shard_map/reduce_scatter | solution.py:123
  134.5 1.4 copy-start.2
  135.3 77.8 %collective-permute-start = (bf16[2,512,128]{1,2,0:T(8,128)(2,1)}, bf16[2,512,128]{1,2,0:T(8,128)(2,1)}, u32[]{:S(2)}, u32[]{:S(2)}) collective-permute-start(bf16[2,512,128]{1,2,0:T(8,128)(2,1)} %pad_maximum_fusion.1), channel_id=1, source_target_pairs={{0,16},{16,0},{1,17},{17,1},{2,18},{18,2},{3,19},{19,3},{4,20},{20... | collective-permute-start | bytes 786440 | tf_op jit(solution)/shard_map/while/body/eval_jaxpr/ppermute | solution.py:15
  215.2 2.3 copy-start.3
  285.5 42.8 %copy-start = (bf16[1,512,1024]{2,1,0:T(8,128)(2,1)S(1)}, bf16[1,512,1024]{2,1,0:T(8,128)(2,1)}, u32[]{:S(2)}) copy-start(bf16[1,512,1024]{2,1,0:T(8,128)(2,1)} %param.8) | copy-start | bytes 3145732
  285.5 42.8 %copy-start.1 = (bf16[1,512,1024]{2,1,0:T(8,128)(2,1)S(1)}, bf16[1,512,1024]{2,1,0:T(8,128)(2,1)}, u32[]{:S(2)}) copy-start(bf16[1,512,1024]{2,1,0:T(8,128)(2,1)} %param.9) | copy-start | bytes 3145732
Sparse Core Ops, SparseCore 0:
  9.5 37.1 all-gather.14
  48.9 40.2 all-gather.6
  91.3 39.0 all-gather.10
  132.4 71.5 all-gather.8
  205.8 73.1 all-gather.12
  285.7 42.5 reduce-scatter.1
where the time goes:
time: 379 us
  waiting for transfers between devices  281 us (74%)
  blocking collectives  39.5 us (10%)
  matrix products  27.6 us (7%)
  between operations  16.1 us (4%)
  other arithmetic  13.3 us (4%)
    all_gather x1, waiting for transfers between devices, on_device(): lax.all_gather(w_query, ('ctx', 'dp'), axis=0, tiled=True)  68.1 us
    all_gather x1, waiting for transfers between devices, on_device(): lax.all_gather(w_out, ('ctx', 'dp'), axis=1, tiled=True)  57.8 us
    reduce_scatter x1, waiting for transfers between devices, on_device(): lax.psum_scatter(terms.astype(jnp.bfloat16), 'tp', scatter_dimension=1, t...  42.7 us
    psum x1, blocking collectives, on_device(): squares = lax.psum(jnp.sum(resid * resid), ('ctx', 'tp', 'dp'))  39.5 us
    all_gather x1, waiting for transfers between devices, on_device(): lax.all_gather(w_key, ('ctx', 'dp'), axis=0, tiled=True)  39.3 us
    all_gather x1, waiting for transfers between devices, on_device(): lax.all_gather(value_matrix, ('ctx', 'dp'), axis=0, tiled=True)  36.5 us
    all_gather x1, waiting for transfers between devices, on_device(): whole = lax.all_gather(local, 'tp', axis=1, tiled=True)  33.2 us
    dot_general x3, matrix products, on_device(): jnp.dot(normed, piece, preferred_element_type=jnp.float32)  14.1 us
  transfers between devices with their start and end apart: 7, of which 6 were waited for; matrix products, arithmetic and copies ran while one was open for 9% of the time, Pallas kernels for 0%

commit v1 on v0

--- a/solution.py
+++ b/solution.py
@@ -66,10 +66,23 @@
     normed = (
         wide * lax.rsqrt(jnp.mean(wide * wide, axis=1, keepdims=True) + 1e-05) * gain[None, :]
     ).astype(jnp.bfloat16)
+
+    def serve_spans(xin, shard_axis, array_dim):
+        carry_in = jnp.concatenate(
+            lax.all_to_all(
+                jnp.stack(tuple((xin for _ in range(lax.axis_size(shard_axis)))), 0),
+                shard_axis,
+                0,
+                0,
+            ),
+            axis=array_dim,
+        )
+        return carry_in
+
     pieces = (
         lax.all_gather(w_query, ("ctx", "dp"), axis=0, tiled=True),
         lax.all_gather(w_key, ("ctx", "dp"), axis=0, tiled=True),
-        lax.all_gather(value_matrix, ("ctx", "dp"), axis=0, tiled=True),
+        serve_spans(value_matrix, ("ctx", "dp"), 0),
     )
     query_rows, key, value_rows = tuple(
         (jnp.dot(normed, piece, preferred_element_type=jnp.float32) for piece in pieces)

time: 379 us -> 339 us (0.89)
  waiting for transfers between devices: 281 us -> 232 us
  starting transfers between devices: 0.82 us -> 8.19 us
    all_gather x1 -> x0, waiting for transfers between devices: 36.5 us -> none  [on_device(): lax.all_gather(value_matrix, ('ctx', 'dp'), axis=0, tiled=True)]
    all_gather x1, waiting for transfers between devices: 33.2 us -> 25 us  [on_device(): whole = lax.all_gather(local, 'tp', axis=1, tiled=True)]
    all_to_all x0 -> x1, starting transfers between devices: none -> 7.41 us  [serve_spans(): lax.all_to_all(jnp.stack(tuple((xin for _ in range(lax.axis_size(shard_ax...]
  transfers between devices with their start and end apart: 7 -> 7, of which waited for: 6 -> 5; matrix products, arithmetic and copies ran while one was open for 9% -> 10% of each run, Pallas kernels for 0% -> 0%
where the time goes in v1:
time: 339 us; the launch traced here: 338 us
  waiting for transfers between devices  232 us (68%)
  blocking collectives  39.5 us (12%)
  matrix products  27.2 us (8%)
  between operations  15.8 us (5%)
  other arithmetic  12.6 us (4%)
  starting transfers between devices  8.19 us (2%)
    all_gather x1, waiting for transfers between devices, on_device(): lax.all_gather(w_query, ('ctx', 'dp'), axis=0, tiled=True)  64.8 us
    all_gather x1, waiting for transfers between devices, on_device(): lax.all_gather(w_out, ('ctx', 'dp'), axis=1, tiled=True)  57.9 us
    reduce_scatter x1, waiting for transfers between devices, on_device(): lax.psum_scatter(terms.astype(jnp.bfloat16), 'tp', scatter_dimension=1, t...  42.7 us
    psum x1, blocking collectives, on_device(): squares = lax.psum(jnp.sum(resid * resid), ('ctx', 'tp', 'dp'))  39.5 us
    all_gather x1, waiting for transfers between devices, on_device(): lax.all_gather(w_key, ('ctx', 'dp'), axis=0, tiled=True)  39.3 us
    all_gather x1, waiting for transfers between devices, on_device(): whole = lax.all_gather(local, 'tp', axis=1, tiled=True)  25 us
    dot_general x3, matrix products, on_device(): jnp.dot(normed, piece, preferred_element_type=jnp.float32)  13.8 us
    all_to_all x1, starting transfers between devices, serve_spans(): lax.all_to_all(jnp.stack(tuple((xin for _ in range(lax.axis_size(shard_ax...  7.41 us
  transfers between devices with their start and end apart: 7, of which 5 were waited for; matrix products, arithmetic and copies ran while one was open for 10% of the time, Pallas kernels for 0%

profile of v1, /device:TPU:0, one launch (start us, length us, event | category | flops | bytes accessed | tf_op | source)
XLA Modules:
  0.0 338.3 jit_solution(3174210367991846716)
XLA Ops:
  7.2 0.7 all-gather.12.cloned.1.call-update
  8.0 0.7 all-gather.6.cloned.1.call-update
  8.7 0.7 all-gather.8.cloned.1.call-update
  9.4 2.0 stack.6
  11.4 7.4 %all-to-all-start = ((bf16[8,512,128]{2,1,0:T(8,128)(2,1)}), bf16[8,512,128]{2,1,0:T(8,128)(2,1)S(1)}, u32[]{:S(2)}, u32[]{:S(2)}) async-start(bf16[8,512,128]{2,1,0:T(8,128)(2,1)} %stack.6), calls=%async_computation | async-start | bytes 2097152 | tf_op jit(solution)/shard_map/all_to_all | solution.py:72
  18.9 0.5 all-gather.10.cloned.1.call-update
  19.6 1.8 multiply_cosine_fusion
  21.4 0.4 broadcast_compare_fusion
  21.8 25.0 %all-gather.12.cloned.1.call-done = bf16[1,512,4096]{2,1,0:T(8,128)(2,1)} async-done(((bf16[1,512,1024]{2,1,0:T(8,128)(2,1)}), bf16[1,512,4096]{2,1,0:T(8,128)(2,1)}) %all-gather.12.cloned.1.call-update) | async-done | bytes 4194320 | tf_op jit(solution)/shard_map/all_gather | solution.py:64
  46.8 3.1 fusion
  49.9 39.3 %all-gather.6.cloned.1.call-done = bf16[4096,128]{1,0:T(8,128)(2,1)} async-done(((bf16[512,128]{1,0:T(8,128)(2,1)}), bf16[4096,128]{1,0:T(8,128)(2,1)}) %all-gather.6.cloned.1.call-update) | async-done | bytes 1048592 | tf_op jit(solution)/shard_map/all_gather | solution.py:84
  89.2 4.1 %convolution_bitcast_fusion = f32[512,1,128]{0,2,1:T(8,128)S(1)} fusion(bf16[4096,128]{1,0:T(8,128)(2,1)} %all-gather.6.cloned.1.call-done, bf16[1,512,4096]{2,1,0:T(8,128)(2,1)} %all-gather.12.cloned.1.call-done, f32[4096]{0:T(1024)S(1)} %copy-done.5, f32[512]{0:T(512)S(1)} %add_rsqrt_fusion), kind=kOutput, calls=%fused_computation.31 | convolution fusion | flops 545259520 | bytes 5523456 | tf_op jit(solution)/shard_map/dot_general | solution.py:88
  93.3 0.6 fusion.41
  93.9 3.8 %convolution_convert_fusion.1 = bf16[512,128]{0,1:T(8,128)(2,1)S(1)} fusion(bf16[4096,128]{1,0:T(8,128)(2,1)S(1)} %bitcast.167, bf16[1,512,4096]{2,1,0:T(8,128)(2,1)} %all-gather.12.cloned.1.call-done, f32[4096]{0:T(1024)S(1)} %copy-done.5, f32[512]{0:T(512)S(1)} %add_rsqrt_fusion), kind=kOutput, calls=%fused_computation.32 | convolution fusion | flops 545325056 | bytes 5392384 | tf_op jit(solution)/shard_map/dot_general | solution.py:88
  97.7 0.7 pad_maximum_fusion.1
  98.4 0.6 collective-permute-start
  99.0 64.8 %all-gather.8.cloned.1.call-done = bf16[4096,512]{1,0:T(8,128)(2,1)} async-done(((bf16[512,512]{1,0:T(8,128)(2,1)}), bf16[4096,512]{1,0:T(8,128)(2,1)}) %all-gather.8.cloned.1.call-update) | async-done | bytes 4194320 | tf_op jit(solution)/shard_map/all_gather | solution.py:83
  163.8 5.9 %fusion.74 = f32[512,512]{0,1:T(8,128)S(1)} fusion(bf16[4096,512]{1,0:T(8,128)(2,1)} %all-gather.8.cloned.1.call-done, bf16[1,512,4096]{2,1,0:T(8,128)(2,1)} %all-gather.12.cloned.1.call-done, f32[4096]{0:T(1024)S(1)} %copy-done.5, f32[512]{0:T(512)S(1)} %add_rsqrt_fusion), kind=kOutput, calls=%fused_computation.109 | convolution fusion | flops 2155872256 | bytes 9455616 | tf_op jit(solution)/shard_map/dot_general | solution.py:88
  169.8 0.3 copy.31
  170.1 0.3 copy.32
  170.5 1.2 subtract_convert_fusion
  171.7 1.2 fusion.3
  173.0 2.1 fusion.4
  175.1 1.0 fusion.5
  176.1 1.2 fusion.7
  177.4 1.3 fusion.28
  178.8 2.2 divide_convert_fusion
  181.0 57.9 %all-gather.10.cloned.1.call-done = bf16[512,4096]{1,0:T(8,128)(2,1)} async-done(((bf16[512,512]{1,0:T(8,128)(2,1)}), bf16[512,4096]{1,0:T(8,128)(2,1)}) %all-gather.10.cloned.1.call-update) | async-done | bytes 4194320 | tf_op jit(solution)/shard_map/all_gather | solution.py:133
  238.8 6.5 %convolution_convert_fusion = bf16[512,4096]{1,0:T(8,128)(2,1)} fusion(bf16[512,512]{0,1:T(8,128)(2,1)S(1)} %bitcast.174, bf16[512,4096]{1,0:T(8,128)(2,1)} %all-gather.10.cloned.1.call-done), kind=kOutput, calls=%fused_computation.5 | convolution fusion | flops 2149580800 | bytes 8912896 | tf_op jit(solution)/shard_map/dot_general | solution.py:131
  245.4 42.7 %reduce-scatter.2.cloned.1.call-done = bf16[512,1024]{1,0:T(8,128)(2,1)} async-done(((bf16[512,4096]{1,0:T(8,128)(2,1)}), bf16[512,1024]{1,0:T(8,128)(2,1)}) %reduce-scatter.2.cloned.1.call-update) | async-done | bytes 1048592 | tf_op jit(solution)/shard_map/reduce_scatter | solution.py:136
  288.1 2.4 fusion.12
  290.5 39.5 %psum.7 = f32[]{:T(128)} all-reduce(f32[]{:T(128)} %fusion.12), channel_id=1, replica_groups=mesh['ctx'=2,'tp'=4,'dp'=4] {'ctx','tp','dp'}, use_global_device_ids=true, to_apply=%region_9.10 | all-reduce | flops 1 | bytes 8 | tf_op jit(solution)/shard_map/psum | solution.py:138
  (29 shorter events, 0.5 us)
Async XLA Ops:
  7.2 12.3 %copy-start.4 = (s32[4]{0:T(128)S(1)}, s32[4]{0:T(128)}, u32[]{:S(2)}) copy-start(s32[4]{0:T(128)} %param.15) | copy-start | bytes 52
  7.2 39.6 %all-gather.12.cloned.1.call-start = ((), (), s32[]{:S(2)}) async-start(), calls=%async_computation.6 | async-start | bytes 5242880 | tf_op jit(solution)/shard_map/all_gather | solution.py:64
  7.9 81.3 %all-gather.6.cloned.1.call-start = ((), (), s32[]{:S(2)}) async-start(), calls=%async_computation.2 | async-start | bytes 1179648 | tf_op jit(solution)/shard_map/all_gather | solution.py:84
  8.7 155.1 %all-gather.8.cloned.1.call-start = ((), (), s32[]{:S(2)}) async-start(), calls=%async_computation.3 | async-start | bytes 4718592 | tf_op jit(solution)/shard_map/all_gather | solution.py:83
  11.4 77.8 %copy-start.5 = (f32[4096]{0:T(1024)S(1)}, f32[4096]{0:T(1024)}, u32[]{:S(2)}) copy-start(f32[4096]{0:T(1024)} %param.10) | copy-start | bytes 49156
  11.4 82.5 %all-to-all-start = ((bf16[8,512,128]{2,1,0:T(8,128)(2,1)}), bf16[8,512,128]{2,1,0:T(8,128)(2,1)S(1)}, u32[]{:S(2)}, u32[]{:S(2)}) async-start(bf16[8,512,128]{2,1,0:T(8,128)(2,1)} %stack.6), calls=%async_computation | async-start | bytes 2097152 | tf_op jit(solution)/shard_map/all_to_all | solution.py:72
  18.8 220.0 %all-gather.10.cloned.1.call-start = ((), (), s32[]{:S(2)}) async-start(), calls=%async_computation.4 | async-start | bytes 4718592 | tf_op jit(solution)/shard_map/all_gather | solution.py:133
  19.4 268.8 %reduce-scatter.2.cloned.1.call-start = ((), (), s32[]{:S(2)}) async-start(), calls=%async_computation.5 | async-start | bytes 5242880 | tf_op jit(solution)/shard_map/reduce_scatter | solution.py:136
  97.7 72.1 %copy-start.2 = (bf16[512,128]{0,1:T(8,128)(2,1)}, bf16[512,128]{0,1:T(8,128)(2,1)S(1)}, u32[]{:S(2)}) copy-start(bf16[512,128]{0,1:T(8,128)(2,1)S(1)} %convolution_convert_fusion.1) | copy-start | bytes 393220
  98.4 74.5 %collective-permute-start = (bf16[2,512,128]{1,2,0:T(8,128)(2,1)}, bf16[2,512,128]{1,2,0:T(8,128)(2,1)}, u32[]{:S(2)}, u32[]{:S(2)}) collective-permute-start(bf16[2,512,128]{1,2,0:T(8,128)(2,1)} %pad_maximum_fusion.1), channel_id=1, source_target_pairs={{0,16},{16,0},{1,17},{17,1},{2,18},{18,2},{3,19},{19,3},{4,20},{20... | collective-permute-start | bytes 786440 | tf_op jit(solution)/shard_map/while/body/eval_jaxpr/ppermute | solution.py:15
  175.1 2.3 copy-start.3
  245.4 42.8 %copy-start = (bf16[1,512,1024]{2,1,0:T(8,128)(2,1)S(1)}, bf16[1,512,1024]{2,1,0:T(8,128)(2,1)}, u32[]{:S(2)}) copy-start(bf16[1,512,1024]{2,1,0:T(8,128)(2,1)} %param.8) | copy-start | bytes 3145732
  245.4 42.8 %copy-start.1 = (bf16[1,512,1024]{2,1,0:T(8,128)(2,1)S(1)}, bf16[1,512,1024]{2,1,0:T(8,128)(2,1)}, u32[]{:S(2)}) copy-start(bf16[1,512,1024]{2,1,0:T(8,128)(2,1)} %param.9) | copy-start | bytes 3145732
Sparse Core Ops, SparseCore 0:
  9.5 37.1 all-gather.11
  48.9 40.2 all-gather.5
  91.3 72.4 all-gather.7
  165.6 73.1 all-gather.9
  245.5 42.5 reduce-scatter.1
